TPU v7x, 256 devices: a whole 4x4x8 slice. The times are simulated.
256 devices in a mesh: tm: 16 (over z, core), space: 16 (over y, x).
Axes of the slice: x: 4, y: 4, z: 8, core: 2. Of those that a mesh axis runs over, the one named last changes fastest.
Arguments:
- residual: float32 [64, 32, 128, 128], P('tm', 'space'), may hold values from -6 to 6
- absorption: float32 [32, 128, 128], P('space'), may hold values from 0.05 to 1
- counts: int32 [64], replicated, may hold values from 1 to 6
Outputs:
- preconditioned: float32 [64, 32, 128, 128], P('tm', 'space')
Inputs may be any that keep to these rules, and one draw needn't show every extreme that they name: counts[k] is the number of minimal-residual steps of frequency k.
All inputs are finite; a program needn't handle non-finite values.
Results may differ from a plain program's by a relative error of at most 0.00022.
Values sent between devices are 32-bit elements; how exact they have to be, the bound alone decides.
No kernel may reach another device: no remote copies, remote signals or barrier semaphores. Data moves between devices by JAX's collectives and lax.ppermute only.
A program may use at most 64 MiB of HBM per device.

v0:
```python
import math
import jax
import jax.numpy as jnp
from jax import lax
from jax.sharding import PartitionSpec as P

L = 64
wrap_factor = 0.1
step_size = 1.0
norm_floor = 1e-06
highest = lax.Precision.HIGHEST


def with_halo(cells, sides, width):
    for axis, dim in sides:
        count = lax.axis_size(axis)
        ends = count - 1
        head = lax.slice_in_dim(cells, 0, width, axis=dim)
        tail = lax.slice_in_dim(cells, cells.shape[dim] - width, cells.shape[dim], axis=dim)
        cells = jnp.concatenate(
            [
                lax.ppermute(tail, axis, [(i, (i + 1) % count) for i in range(ends)]),
                cells,
                lax.ppermute(head, axis, [((i + 1) % count, i) for i in range(ends)]),
            ],
            axis=dim,
        )
    return cells


def copy_for_each(shard, axis):
    copies = jnp.broadcast_to(shard, (lax.axis_size(axis), *shard.shape))
    return lax.all_to_all(copies, axis, split_axis=0, concat_axis=0, tiled=True)


def taken_together(shard, axis):
    return copy_for_each(shard, axis).sum(axis=0)


def packed_total(arrays, axis):
    vector, at, finished = (jnp.concatenate([a.reshape(-1) for a in arrays]), 0, [])
    so_far = taken_together(vector, axis)
    for a in arrays:
        finished.append(so_far[at : at + a.size].reshape(a.shape))
        at += a.size
    return tuple(finished)


def shifts(frequency):
    angles = frequency.astype(jnp.float32) * (2.0 * math.pi / L)
    decay_rate = wrap_factor ** (1.0 / L)
    shift_re = (1.0 - decay_rate * jnp.cos(angles)) / step_size
    shift_im = decay_rate * jnp.sin(angles) / step_size
    return (shift_re, shift_im)


def near_sum(padded):
    interior = padded[..., 1:-1, :, :]
    widths = [(0, 0)] * (interior.ndim - 2) + [(1, 1), (1, 1)]
    padded_xy = jnp.pad(interior, widths)
    summed = padded[..., 2:, :, :] + padded[..., :-2, :, :]
    summed = summed + padded_xy[..., 2:, 1:-1] + padded_xy[..., :-2, 1:-1]
    summed = summed + padded_xy[..., 1:-1, 2:] + padded_xy[..., 1:-1, :-2]
    return summed


def advance(carried, dir_re, dir_im, img_re, img_im, coef_re, coef_im):
    sol_re, sol_im, res_re, res_im = carried
    sol_re = sol_re + coef_re * dir_re - coef_im * dir_im
    sol_im = sol_im + coef_re * dir_im + coef_im * dir_re
    res_re = res_re - (coef_re * img_re - coef_im * img_im)
    res_im = res_im - (coef_re * img_im + coef_im * img_re)
    return (sol_re, sol_im, res_re, res_im)


def solve_together(spectrum, absorption, frequencies, step_counts, longest):
    shift_re, shift_im = shifts(frequencies)
    shift_re = shift_re[:, None, None, None]
    shift_im = shift_im[:, None, None, None]
    diag_re = shift_re + 6.0 + absorption[None]
    magnitude = diag_re * diag_re + shift_im * shift_im
    inv_re = diag_re / magnitude
    inv_im = -shift_im / magnitude

    def iterate(iteration, carried):
        res_re, res_im = (carried[2], carried[3])
        dir_re = inv_re * res_re - inv_im * res_im
        dir_im = inv_re * res_im + inv_im * res_re
        padded = with_halo(jnp.stack([dir_re, dir_im], axis=1), (("space", 2),), 1)
        nearby = near_sum(padded)
        img_re = diag_re * dir_re - shift_im * dir_im - nearby[:, 0]
        img_im = diag_re * dir_im + shift_im * dir_re - nearby[:, 1]
        totals = packed_total(
            (
                jnp.sum(img_re * res_re + img_im * res_im, axis=(1, 2, 3)),
                jnp.sum(img_re * res_im - img_im * res_re, axis=(1, 2, 3)),
                jnp.sum(img_re * img_re + img_im * img_im, axis=(1, 2, 3)),
            ),
            "space",
        )
        active = iteration < step_counts
        denominator = totals[2] + norm_floor
        coef_re = jnp.where(active, totals[0] / denominator, 0.0)[:, None, None, None]
        coef_im = jnp.where(active, totals[1] / denominator, 0.0)[:, None, None, None]
        return advance(carried, dir_re, dir_im, img_re, img_im, coef_re, coef_im)

    blank = jnp.zeros_like(spectrum[:, 0])
    finished = lax.fori_loop(0, longest, iterate, (blank, blank, spectrum[:, 0], spectrum[:, 1]))
    return jnp.stack([finished[0], finished[1]], axis=1)


def slot_order():
    return jnp.arange(L, dtype=jnp.int32)


def phase_table(left, right):
    return (left[:, None] * right[None, :] % L).astype(jnp.float32) * (2.0 * math.pi / L)


def body(residual, absorption, counts):
    per_device = residual.shape[0]
    decay_rate = wrap_factor ** (1.0 / L)
    first_step = lax.axis_index("tm") * per_device
    times_here = first_step + jnp.arange(per_device, dtype=jnp.int32)
    scaled = residual * jnp.power(decay_rate, times_here.astype(jnp.float32))[:, None, None, None]
    slot_freqs = slot_order()
    own_freqs = lax.dynamic_slice_in_dim(slot_freqs, first_step, per_device)
    own_counts = counts[own_freqs]
    longest = jnp.max(counts)
    all_times = jnp.arange(L, dtype=jnp.int32)
    series = lax.all_to_all(scaled, "tm", split_axis=2, concat_axis=0, tiled=True)
    phases = phase_table(slot_freqs, all_times)
    real_part = jnp.einsum("sn,nzxy->szxy", jnp.cos(phases), series, precision=highest)
    imag_part = -jnp.einsum("sn,nzxy->szxy", jnp.sin(phases), series, precision=highest)
    spectrum = lax.all_to_all(
        jnp.stack([real_part, imag_part], axis=1), "tm", split_axis=0, concat_axis=3, tiled=True
    )
    solved = solve_together(spectrum, absorption, own_freqs, own_counts, longest)
    gathered = lax.all_to_all(solved, "tm", split_axis=3, concat_axis=0, tiled=True)
    phases = phase_table(all_times, slot_freqs)
    values = jnp.einsum("ns,szxy->nzxy", jnp.cos(phases), gathered[:, 0], precision=highest)
    values = values - jnp.einsum(
        "ns,szxy->nzxy", jnp.sin(phases), gathered[:, 1], precision=highest
    )
    weight = jnp.power(decay_rate, -all_times.astype(jnp.float32)) / L
    values = values * weight[:, None, None, None]
    return lax.all_to_all(values, "tm", split_axis=0, concat_axis=2, tiled=True)


def solution(mesh):
    in_specs = (P("tm", "space", None, None), P("space", None, None), P())
    out_specs = P("tm", "space", None, None)
    return jax.shard_map(body, mesh=mesh, in_specs=in_specs, out_specs=out_specs, check_vma=False)
```

profile of v0, /device:TPU:1, one launch (start us, length us, event | category | flops | bytes accessed | tf_op | source)
XLA Modules:
  0.0 341.6 jit_solution(1226429195683885706)
XLA Ops:
  1.5 27.0 %all_to_all.84 = f32[4,2,128,128]{3,0,1,2:T(4,128)S(1)} all-to-all(f32[4,2,128,128]{3,0,1,2:T(4,128)S(1)} %copy.60), channel_id=1, replica_groups=mesh['tm'=16,'space'=16] {'tm'}, dimensions={2} | all-to-all | bytes 1048576 | tf_op jit(solution)/shard_map/all_to_all | solution.py:131
  30.2 1.6 copy.62
  31.8 3.7 %all-to-all-start.2 = ((f32[64,2,2,8,128]{4,3,2,1,0:T(8,128)}), f32[64,2,2,8,128]{4,3,2,1,0:T(8,128)S(1)}, u32[]{:S(2)}, u32[]{:S(2)}) async-start(f32[64,2,2,8,128]{4,3,2,1,0:T(8,128)} %copy.62), calls=%async_computation.2 | async-start | bytes 2097152 | tf_op jit(solution)/shard_map/all_to_all | solution.py:135
  37.0 25.8 %all-to-all-done.2 = f32[64,2,2,8,128]{4,3,2,1,0:T(8,128)S(1)} async-done(((f32[64,2,2,8,128]{4,3,2,1,0:T(8,128)}), f32[64,2,2,8,128]{4,3,2,1,0:T(8,128)S(1)}, u32[]{:S(2)}, u32[]{:S(2)}) %all-to-all-start.2) | async-done | bytes 1048608 | tf_op jit(solution)/shard_map/all_to_all | solution.py:135
  64.7 204.2 %while.20 = (s32[]{:T(128)}, f32[4,2,128,128]{3,2,1,0:T(8,128)}, f32[4,2,128,128]{3,2,1,0:T(8,128)}, f32[4,2,128,128]{3,2,1,0:T(8,128)S(1)}, f32[4,2,128,128]{3,...) while((s32[]{:T(128)}, f32[4,2,128,128]{3,2,1,0:T(8,128)}, ...), condition=%wide.region_6.7_spmd.clone.clone, body=%wide.region_1.6_spmd.clone.clone.sunk | while | flops 9175258 | bytes 25447364 | solution.py:108
  65.8 3.2 collective-permute-start
  70.3 9.4 %collective-permute-done = f32[4,2,1,128,128]{4,3,2,0,1:T(8,128)S(1)} collective-permute-done((f32[4,2,1,128,128]{4,3,2,0,1:T(8,128)S(1)}, f32[4,2,1,128,128]{4,3,2,0,1:T(8,128)S(1)}, u32[]{:S(2)}, u32[]{:S(2)}) %collective-permute-start) | collective-permute-done | bytes 524320 | tf_op jit(solution)/shard_map/while/body/ppermute | solution.py:22
  79.8 4.1 %collective-permute-done.1 = f32[4,2,1,128,128]{4,3,2,0,1:T(8,128)S(1)} collective-permute-done((f32[4,2,1,128,128]{4,3,2,0,1:T(8,128)S(1)}, f32[4,2,1,128,128]{4,3,2,0,1:T(8,128)S(1)}, u32[]{:S(2)}, u32[]{:S(2)}) %collective-permute-start.1) | collective-permute-done | bytes 524320 | tf_op jit(solution)/shard_map/while/body/ppermute | solution.py:24
  85.9 8.3 %all-to-all-start = ((f32[16,1,12]{2,1,0:T(1,128)}), f32[16,1,12]{2,1,0:T(1,128)S(1)}, u32[]{:S(2)}, u32[]{:S(2)}) async-start(f32[16,1,12]{2,1,0:T(1,128)} %broadcast_in_dim.42), calls=%async_computation | async-start | bytes 16384 | tf_op jit(solution)/shard_map/while/body/all_to_all | solution.py:33
  94.2 6.4 %all-to-all-done = f32[16,1,12]{2,1,0:T(1,128)S(1)} async-done(((f32[16,1,12]{2,1,0:T(1,128)}), f32[16,1,12]{2,1,0:T(1,128)S(1)}, u32[]{:S(2)}, u32[]{:S(2)}) %all-to-all-start) | async-done | bytes 800 | tf_op jit(solution)/shard_map/while/body/all_to_all | solution.py:33
  100.7 2.8 add_subtract_fusion.2
  104.6 2.1 collective-permute-start
  106.7 1.3 collective-permute-start.1
  108.1 8.1 %collective-permute-done = f32[4,2,1,128,128]{4,3,2,0,1:T(8,128)S(1)} collective-permute-done((f32[4,2,1,128,128]{4,3,2,0,1:T(8,128)S(1)}, f32[4,2,1,128,128]{4,3,2,0,1:T(8,128)S(1)}, u32[]{:S(2)}, u32[]{:S(2)}) %collective-permute-start) | collective-permute-done | bytes 524320 | tf_op jit(solution)/shard_map/while/body/ppermute | solution.py:22
  116.2 3.9 %collective-permute-done.1 = f32[4,2,1,128,128]{4,3,2,0,1:T(8,128)S(1)} collective-permute-done((f32[4,2,1,128,128]{4,3,2,0,1:T(8,128)S(1)}, f32[4,2,1,128,128]{4,3,2,0,1:T(8,128)S(1)}, u32[]{:S(2)}, u32[]{:S(2)}) %collective-permute-start.1) | collective-permute-done | bytes 524320 | tf_op jit(solution)/shard_map/while/body/ppermute | solution.py:24
  122.1 7.8 %all-to-all-start = ((f32[16,1,12]{2,1,0:T(1,128)}), f32[16,1,12]{2,1,0:T(1,128)S(1)}, u32[]{:S(2)}, u32[]{:S(2)}) async-start(f32[16,1,12]{2,1,0:T(1,128)} %broadcast_in_dim.42), calls=%async_computation | async-start | bytes 16384 | tf_op jit(solution)/shard_map/while/body/all_to_all | solution.py:33
  129.9 6.4 %all-to-all-done = f32[16,1,12]{2,1,0:T(1,128)S(1)} async-done(((f32[16,1,12]{2,1,0:T(1,128)}), f32[16,1,12]{2,1,0:T(1,128)S(1)}, u32[]{:S(2)}, u32[]{:S(2)}) %all-to-all-start) | async-done | bytes 800 | tf_op jit(solution)/shard_map/while/body/all_to_all | solution.py:33
  136.4 2.8 add_subtract_fusion.2
  140.3 2.1 collective-permute-start
  143.8 5.7 %collective-permute-done = f32[4,2,1,128,128]{4,3,2,0,1:T(8,128)S(1)} collective-permute-done((f32[4,2,1,128,128]{4,3,2,0,1:T(8,128)S(1)}, f32[4,2,1,128,128]{4,3,2,0,1:T(8,128)S(1)}, u32[]{:S(2)}, u32[]{:S(2)}) %collective-permute-start) | collective-permute-done | bytes 524320 | tf_op jit(solution)/shard_map/while/body/ppermute | solution.py:22
  149.5 3.9 %collective-permute-done.1 = f32[4,2,1,128,128]{4,3,2,0,1:T(8,128)S(1)} collective-permute-done((f32[4,2,1,128,128]{4,3,2,0,1:T(8,128)S(1)}, f32[4,2,1,128,128]{4,3,2,0,1:T(8,128)S(1)}, u32[]{:S(2)}, u32[]{:S(2)}) %collective-permute-start.1) | collective-permute-done | bytes 524320 | tf_op jit(solution)/shard_map/while/body/ppermute | solution.py:24
  155.3 7.8 %all-to-all-start = ((f32[16,1,12]{2,1,0:T(1,128)}), f32[16,1,12]{2,1,0:T(1,128)S(1)}, u32[]{:S(2)}, u32[]{:S(2)}) async-start(f32[16,1,12]{2,1,0:T(1,128)} %broadcast_in_dim.42), calls=%async_computation | async-start | bytes 16384 | tf_op jit(solution)/shard_map/while/body/all_to_all | solution.py:33
  163.2 6.4 %all-to-all-done = f32[16,1,12]{2,1,0:T(1,128)S(1)} async-done(((f32[16,1,12]{2,1,0:T(1,128)}), f32[16,1,12]{2,1,0:T(1,128)S(1)}, u32[]{:S(2)}, u32[]{:S(2)}) %all-to-all-start) | async-done | bytes 800 | tf_op jit(solution)/shard_map/while/body/all_to_all | solution.py:33
  169.7 2.8 add_subtract_fusion.2
  173.6 2.1 collective-permute-start
  175.6 1.3 collective-permute-start.1
  177.0 4.7 %collective-permute-done = f32[4,2,1,128,128]{4,3,2,0,1:T(8,128)S(1)} collective-permute-done((f32[4,2,1,128,128]{4,3,2,0,1:T(8,128)S(1)}, f32[4,2,1,128,128]{4,3,2,0,1:T(8,128)S(1)}, u32[]{:S(2)}, u32[]{:S(2)}) %collective-permute-start) | collective-permute-done | bytes 524320 | tf_op jit(solution)/shard_map/while/body/ppermute | solution.py:22
  181.7 3.8 %collective-permute-done.1 = f32[4,2,1,128,128]{4,3,2,0,1:T(8,128)S(1)} collective-permute-done((f32[4,2,1,128,128]{4,3,2,0,1:T(8,128)S(1)}, f32[4,2,1,128,128]{4,3,2,0,1:T(8,128)S(1)}, u32[]{:S(2)}, u32[]{:S(2)}) %collective-permute-start.1) | collective-permute-done | bytes 524320 | tf_op jit(solution)/shard_map/while/body/ppermute | solution.py:24
  187.6 7.5 %all-to-all-start = ((f32[16,1,12]{2,1,0:T(1,128)}), f32[16,1,12]{2,1,0:T(1,128)S(1)}, u32[]{:S(2)}, u32[]{:S(2)}) async-start(f32[16,1,12]{2,1,0:T(1,128)} %broadcast_in_dim.42), calls=%async_computation | async-start | bytes 16384 | tf_op jit(solution)/shard_map/while/body/all_to_all | solution.py:33
  195.1 6.4 %all-to-all-done = f32[16,1,12]{2,1,0:T(1,128)S(1)} async-done(((f32[16,1,12]{2,1,0:T(1,128)}), f32[16,1,12]{2,1,0:T(1,128)S(1)}, u32[]{:S(2)}, u32[]{:S(2)}) %all-to-all-start) | async-done | bytes 800 | tf_op jit(solution)/shard_map/while/body/all_to_all | solution.py:33
  201.6 2.8 add_subtract_fusion.2
  205.5 2.1 collective-permute-start
  209.0 4.7 %collective-permute-done = f32[4,2,1,128,128]{4,3,2,0,1:T(8,128)S(1)} collective-permute-done((f32[4,2,1,128,128]{4,3,2,0,1:T(8,128)S(1)}, f32[4,2,1,128,128]{4,3,2,0,1:T(8,128)S(1)}, u32[]{:S(2)}, u32[]{:S(2)}) %collective-permute-start) | collective-permute-done | bytes 524320 | tf_op jit(solution)/shard_map/while/body/ppermute | solution.py:22
  213.6 3.8 %collective-permute-done.1 = f32[4,2,1,128,128]{4,3,2,0,1:T(8,128)S(1)} collective-permute-done((f32[4,2,1,128,128]{4,3,2,0,1:T(8,128)S(1)}, f32[4,2,1,128,128]{4,3,2,0,1:T(8,128)S(1)}, u32[]{:S(2)}, u32[]{:S(2)}) %collective-permute-start.1) | collective-permute-done | bytes 524320 | tf_op jit(solution)/shard_map/while/body/ppermute | solution.py:24
  219.5 7.5 %all-to-all-start = ((f32[16,1,12]{2,1,0:T(1,128)}), f32[16,1,12]{2,1,0:T(1,128)S(1)}, u32[]{:S(2)}, u32[]{:S(2)}) async-start(f32[16,1,12]{2,1,0:T(1,128)} %broadcast_in_dim.42), calls=%async_computation | async-start | bytes 16384 | tf_op jit(solution)/shard_map/while/body/all_to_all | solution.py:33
  227.0 6.4 %all-to-all-done = f32[16,1,12]{2,1,0:T(1,128)S(1)} async-done(((f32[16,1,12]{2,1,0:T(1,128)}), f32[16,1,12]{2,1,0:T(1,128)S(1)}, u32[]{:S(2)}, u32[]{:S(2)}) %all-to-all-start) | async-done | bytes 800 | tf_op jit(solution)/shard_map/while/body/all_to_all | solution.py:33
  233.5 2.8 add_subtract_fusion.2
  237.4 2.1 collective-permute-start
  240.9 4.7 %collective-permute-done = f32[4,2,1,128,128]{4,3,2,0,1:T(8,128)S(1)} collective-permute-done((f32[4,2,1,128,128]{4,3,2,0,1:T(8,128)S(1)}, f32[4,2,1,128,128]{4,3,2,0,1:T(8,128)S(1)}, u32[]{:S(2)}, u32[]{:S(2)}) %collective-permute-start) | collective-permute-done | bytes 524320 | tf_op jit(solution)/shard_map/while/body/ppermute | solution.py:22
  245.6 3.8 %collective-permute-done.1 = f32[4,2,1,128,128]{4,3,2,0,1:T(8,128)S(1)} collective-permute-done((f32[4,2,1,128,128]{4,3,2,0,1:T(8,128)S(1)}, f32[4,2,1,128,128]{4,3,2,0,1:T(8,128)S(1)}, u32[]{:S(2)}, u32[]{:S(2)}) %collective-permute-start.1) | collective-permute-done | bytes 524320 | tf_op jit(solution)/shard_map/while/body/ppermute | solution.py:24
  251.4 7.5 %all-to-all-start = ((f32[16,1,12]{2,1,0:T(1,128)}), f32[16,1,12]{2,1,0:T(1,128)S(1)}, u32[]{:S(2)}, u32[]{:S(2)}) async-start(f32[16,1,12]{2,1,0:T(1,128)} %broadcast_in_dim.42), calls=%async_computation | async-start | bytes 16384 | tf_op jit(solution)/shard_map/while/body/all_to_all | solution.py:33
  258.9 6.4 %all-to-all-done = f32[16,1,12]{2,1,0:T(1,128)S(1)} async-done(((f32[16,1,12]{2,1,0:T(1,128)}), f32[16,1,12]{2,1,0:T(1,128)S(1)}, u32[]{:S(2)}, u32[]{:S(2)}) %all-to-all-start) | async-done | bytes 800 | tf_op jit(solution)/shard_map/while/body/all_to_all | solution.py:33
  265.5 2.8 add_subtract_fusion.2
  268.9 2.0 copy_bitcast_fusion.2
  270.9 1.5 pad_maximum_fusion.7
  272.4 17.8 %all-to-all-start.3 = ((f32[4,2,2,128,128]{4,2,0,1,3:T(2,128)}), f32[4,2,2,128,128]{4,2,0,1,3:T(2,128)S(1)}, u32[]{:S(2)}, u32[]{:S(2)}) async-start(f32[4,2,2,128,128]{4,2,0,1,3:T(2,128)} %pad_maximum_fusion.7), calls=%async_computation.3 | async-start | bytes 2097152 | tf_op jit(solution)/shard_map/all_to_all | solution.py:139
  290.2 28.0 %all-to-all-done.3 = f32[4,2,2,128,128]{4,2,0,1,3:T(2,128)S(1)} async-done(((f32[4,2,2,128,128]{4,2,0,1,3:T(2,128)}), f32[4,2,2,128,128]{4,2,0,1,3:T(2,128)S(1)}, u32[]{:S(2)}, u32[]{:S(2)}) %all-to-all-start.3) | async-done | bytes 1048608 | tf_op jit(solution)/shard_map/all_to_all | solution.py:139
  320.3 20.4 %all_to_all.85 = f32[64,2,8,128]{3,2,1,0:T(8,128)S(1)} all-to-all(f32[64,2,8,128]{3,2,1,0:T(8,128)S(1)} %copy.67), channel_id=1, replica_groups=mesh['tm'=16,'space'=16] {'tm'}, dimensions={0} | all-to-all | bytes 1048576 | tf_op jit(solution)/shard_map/all_to_all | solution.py:147
  (86 shorter events, 30.0 us)
Async XLA Ops:
  31.8 3.9 %copy-start = (s32[64]{0:T(128)S(1)}, s32[64]{0:T(128)}, u32[]{:S(2)}) copy-start(s32[64]{0:T(128)} %param.7) | copy-start | bytes 772
  31.8 31.0 %all-to-all-start.2 = ((f32[64,2,2,8,128]{4,3,2,1,0:T(8,128)}), f32[64,2,2,8,128]{4,3,2,1,0:T(8,128)S(1)}, u32[]{:S(2)}, u32[]{:S(2)}) async-start(f32[64,2,2,8,128]{4,3,2,1,0:T(8,128)} %copy.62), calls=%async_computation.2 | async-start | bytes 2097152 | tf_op jit(solution)/shard_map/all_to_all | solution.py:135
  63.0 1.7 copy-start.1
  65.8 14.0 %collective-permute-start = (f32[4,2,1,128,128]{4,3,2,0,1:T(8,128)S(1)}, f32[4,2,1,128,128]{4,3,2,0,1:T(8,128)S(1)}, u32[]{:S(2)}, u32[]{:S(2)}) collective-permute-start(f32[4,2,1,128,128]{4,3,2,0,1:T(8,128)S(1)} %get-tuple-element.368), channel_id=1, source_target_pairs={{0,1},{1,2},{2,3},{3,4},{4,5},{5,6},{6,7},{7,8},{8,9},{9,10},{10,1... | collective-permute-start | bytes 1572872 | tf_op jit(solution)/shard_map/while/body/ppermute | solution.py:22
  68.9 15.0 %collective-permute-start.1 = (f32[4,2,1,128,128]{4,3,2,0,1:T(8,128)S(1)}, f32[4,2,1,128,128]{4,3,2,0,1:T(8,128)S(1)}, u32[]{:S(2)}, u32[]{:S(2)}) collective-permute-start(f32[4,2,1,128,128]{4,3,2,0,1:T(8,128)S(1)} %get-tuple-element.369), channel_id=1, source_target_pairs={{1,0},{2,1},{3,2},{4,3},{5,4},{6,5},{7,6},{8,7},{9,8},{10,9},{11,1... | collective-permute-start | bytes 1572872 | tf_op jit(solution)/shard_map/while/body/ppermute | solution.py:24
  85.9 14.7 %all-to-all-start = ((f32[16,1,12]{2,1,0:T(1,128)}), f32[16,1,12]{2,1,0:T(1,128)S(1)}, u32[]{:S(2)}, u32[]{:S(2)}) async-start(f32[16,1,12]{2,1,0:T(1,128)} %broadcast_in_dim.42), calls=%async_computation | async-start | bytes 16384 | tf_op jit(solution)/shard_map/while/body/all_to_all | solution.py:33
  104.6 11.6 %collective-permute-start = (f32[4,2,1,128,128]{4,3,2,0,1:T(8,128)S(1)}, f32[4,2,1,128,128]{4,3,2,0,1:T(8,128)S(1)}, u32[]{:S(2)}, u32[]{:S(2)}) collective-permute-start(f32[4,2,1,128,128]{4,3,2,0,1:T(8,128)S(1)} %get-tuple-element.368), channel_id=1, source_target_pairs={{0,1},{1,2},{2,3},{3,4},{4,5},{5,6},{6,7},{7,8},{8,9},{9,10},{10,1... | collective-permute-start | bytes 1572872 | tf_op jit(solution)/shard_map/while/body/ppermute | solution.py:22
  106.7 13.4 %collective-permute-start.1 = (f32[4,2,1,128,128]{4,3,2,0,1:T(8,128)S(1)}, f32[4,2,1,128,128]{4,3,2,0,1:T(8,128)S(1)}, u32[]{:S(2)}, u32[]{:S(2)}) collective-permute-start(f32[4,2,1,128,128]{4,3,2,0,1:T(8,128)S(1)} %get-tuple-element.369), channel_id=1, source_target_pairs={{1,0},{2,1},{3,2},{4,3},{5,4},{6,5},{7,6},{8,7},{9,8},{10,9},{11,1... | collective-permute-start | bytes 1572872 | tf_op jit(solution)/shard_map/while/body/ppermute | solution.py:24
  122.1 14.3 %all-to-all-start = ((f32[16,1,12]{2,1,0:T(1,128)}), f32[16,1,12]{2,1,0:T(1,128)S(1)}, u32[]{:S(2)}, u32[]{:S(2)}) async-start(f32[16,1,12]{2,1,0:T(1,128)} %broadcast_in_dim.42), calls=%async_computation | async-start | bytes 16384 | tf_op jit(solution)/shard_map/while/body/all_to_all | solution.py:33
  140.3 9.2 %collective-permute-start = (f32[4,2,1,128,128]{4,3,2,0,1:T(8,128)S(1)}, f32[4,2,1,128,128]{4,3,2,0,1:T(8,128)S(1)}, u32[]{:S(2)}, u32[]{:S(2)}) collective-permute-start(f32[4,2,1,128,128]{4,3,2,0,1:T(8,128)S(1)} %get-tuple-element.368), channel_id=1, source_target_pairs={{0,1},{1,2},{2,3},{3,4},{4,5},{5,6},{6,7},{7,8},{8,9},{9,10},{10,1... | collective-permute-start | bytes 1572872 | tf_op jit(solution)/shard_map/while/body/ppermute | solution.py:22
  142.4 11.0 %collective-permute-start.1 = (f32[4,2,1,128,128]{4,3,2,0,1:T(8,128)S(1)}, f32[4,2,1,128,128]{4,3,2,0,1:T(8,128)S(1)}, u32[]{:S(2)}, u32[]{:S(2)}) collective-permute-start(f32[4,2,1,128,128]{4,3,2,0,1:T(8,128)S(1)} %get-tuple-element.369), channel_id=1, source_target_pairs={{1,0},{2,1},{3,2},{4,3},{5,4},{6,5},{7,6},{8,7},{9,8},{10,9},{11,1... | collective-permute-start | bytes 1572872 | tf_op jit(solution)/shard_map/while/body/ppermute | solution.py:24
  155.3 14.3 %all-to-all-start = ((f32[16,1,12]{2,1,0:T(1,128)}), f32[16,1,12]{2,1,0:T(1,128)S(1)}, u32[]{:S(2)}, u32[]{:S(2)}) async-start(f32[16,1,12]{2,1,0:T(1,128)} %broadcast_in_dim.42), calls=%async_computation | async-start | bytes 16384 | tf_op jit(solution)/shard_map/while/body/all_to_all | solution.py:33
  173.6 8.2 %collective-permute-start = (f32[4,2,1,128,128]{4,3,2,0,1:T(8,128)S(1)}, f32[4,2,1,128,128]{4,3,2,0,1:T(8,128)S(1)}, u32[]{:S(2)}, u32[]{:S(2)}) collective-permute-start(f32[4,2,1,128,128]{4,3,2,0,1:T(8,128)S(1)} %get-tuple-element.368), channel_id=1, source_target_pairs={{0,1},{1,2},{2,3},{3,4},{4,5},{5,6},{6,7},{7,8},{8,9},{9,10},{10,1... | collective-permute-start | bytes 1572872 | tf_op jit(solution)/shard_map/while/body/ppermute | solution.py:22
  175.6 9.9 %collective-permute-start.1 = (f32[4,2,1,128,128]{4,3,2,0,1:T(8,128)S(1)}, f32[4,2,1,128,128]{4,3,2,0,1:T(8,128)S(1)}, u32[]{:S(2)}, u32[]{:S(2)}) collective-permute-start(f32[4,2,1,128,128]{4,3,2,0,1:T(8,128)S(1)} %get-tuple-element.369), channel_id=1, source_target_pairs={{1,0},{2,1},{3,2},{4,3},{5,4},{6,5},{7,6},{8,7},{9,8},{10,9},{11,1... | collective-permute-start | bytes 1572872 | tf_op jit(solution)/shard_map/while/body/ppermute | solution.py:24
  187.6 14.0 %all-to-all-start = ((f32[16,1,12]{2,1,0:T(1,128)}), f32[16,1,12]{2,1,0:T(1,128)S(1)}, u32[]{:S(2)}, u32[]{:S(2)}) async-start(f32[16,1,12]{2,1,0:T(1,128)} %broadcast_in_dim.42), calls=%async_computation | async-start | bytes 16384 | tf_op jit(solution)/shard_map/while/body/all_to_all | solution.py:33
  205.5 8.2 %collective-permute-start = (f32[4,2,1,128,128]{4,3,2,0,1:T(8,128)S(1)}, f32[4,2,1,128,128]{4,3,2,0,1:T(8,128)S(1)}, u32[]{:S(2)}, u32[]{:S(2)}) collective-permute-start(f32[4,2,1,128,128]{4,3,2,0,1:T(8,128)S(1)} %get-tuple-element.368), channel_id=1, source_target_pairs={{0,1},{1,2},{2,3},{3,4},{4,5},{5,6},{6,7},{7,8},{8,9},{9,10},{10,1... | collective-permute-start | bytes 1572872 | tf_op jit(solution)/shard_map/while/body/ppermute | solution.py:22
  207.6 9.9 %collective-permute-start.1 = (f32[4,2,1,128,128]{4,3,2,0,1:T(8,128)S(1)}, f32[4,2,1,128,128]{4,3,2,0,1:T(8,128)S(1)}, u32[]{:S(2)}, u32[]{:S(2)}) collective-permute-start(f32[4,2,1,128,128]{4,3,2,0,1:T(8,128)S(1)} %get-tuple-element.369), channel_id=1, source_target_pairs={{1,0},{2,1},{3,2},{4,3},{5,4},{6,5},{7,6},{8,7},{9,8},{10,9},{11,1... | collective-permute-start | bytes 1572872 | tf_op jit(solution)/shard_map/while/body/ppermute | solution.py:24
  219.5 14.0 %all-to-all-start = ((f32[16,1,12]{2,1,0:T(1,128)}), f32[16,1,12]{2,1,0:T(1,128)S(1)}, u32[]{:S(2)}, u32[]{:S(2)}) async-start(f32[16,1,12]{2,1,0:T(1,128)} %broadcast_in_dim.42), calls=%async_computation | async-start | bytes 16384 | tf_op jit(solution)/shard_map/while/body/all_to_all | solution.py:33
  237.4 8.2 %collective-permute-start = (f32[4,2,1,128,128]{4,3,2,0,1:T(8,128)S(1)}, f32[4,2,1,128,128]{4,3,2,0,1:T(8,128)S(1)}, u32[]{:S(2)}, u32[]{:S(2)}) collective-permute-start(f32[4,2,1,128,128]{4,3,2,0,1:T(8,128)S(1)} %get-tuple-element.368), channel_id=1, source_target_pairs={{0,1},{1,2},{2,3},{3,4},{4,5},{5,6},{6,7},{7,8},{8,9},{9,10},{10,1... | collective-permute-start | bytes 1572872 | tf_op jit(solution)/shard_map/while/body/ppermute | solution.py:22
  239.5 9.9 %collective-permute-start.1 = (f32[4,2,1,128,128]{4,3,2,0,1:T(8,128)S(1)}, f32[4,2,1,128,128]{4,3,2,0,1:T(8,128)S(1)}, u32[]{:S(2)}, u32[]{:S(2)}) collective-permute-start(f32[4,2,1,128,128]{4,3,2,0,1:T(8,128)S(1)} %get-tuple-element.369), channel_id=1, source_target_pairs={{1,0},{2,1},{3,2},{4,3},{5,4},{6,5},{7,6},{8,7},{9,8},{10,9},{11,1... | collective-permute-start | bytes 1572872 | tf_op jit(solution)/shard_map/while/body/ppermute | solution.py:24
  251.4 14.0 %all-to-all-start = ((f32[16,1,12]{2,1,0:T(1,128)}), f32[16,1,12]{2,1,0:T(1,128)S(1)}, u32[]{:S(2)}, u32[]{:S(2)}) async-start(f32[16,1,12]{2,1,0:T(1,128)} %broadcast_in_dim.42), calls=%async_computation | async-start | bytes 16384 | tf_op jit(solution)/shard_map/while/body/all_to_all | solution.py:33
  272.4 45.9 %all-to-all-start.3 = ((f32[4,2,2,128,128]{4,2,0,1,3:T(2,128)}), f32[4,2,2,128,128]{4,2,0,1,3:T(2,128)S(1)}, u32[]{:S(2)}, u32[]{:S(2)}) async-start(f32[4,2,2,128,128]{4,2,0,1,3:T(2,128)} %pad_maximum_fusion.7), calls=%async_computation.3 | async-start | bytes 2097152 | tf_op jit(solution)/shard_map/all_to_all | solution.py:139
where the time goes:
time: 343 us; the launch traced here: 342 us
  waiting for transfers between devices  153 us (45%)
  starting transfers between devices  89.2 us (26%)
  blocking collectives  47.4 us (14%)
  other arithmetic  32 us (9%)
  local copies, waits for them, and re-layouts  11.6 us (3%)
  loops' own time  5.21 us (2%)
    all_to_all x6, starting transfers between devices, copy_for_each(): return lax.all_to_all(copies, axis, split_axis=0, concat_axis=0, tiled=True)  46.4 us
    all_to_all x6, waiting for transfers between devices, copy_for_each(): return lax.all_to_all(copies, axis, split_axis=0, concat_axis=0, tiled=True)  38.6 us
    ppermute x6, waiting for transfers between devices, with_halo(): lax.ppermute(tail, axis, [(i, (i + 1) % count) for i in range(ends)])  37.3 us
    all_to_all x1, waiting for transfers between devices, body(): lax.all_to_all(solved, 'tm', split_axis=3, concat_axis=0, tiled=True)  28 us
    all_to_all x1, blocking collectives, body(): lax.all_to_all(scaled, 'tm', split_axis=2, concat_axis=0, tiled=True)  27 us
    all_to_all x1, waiting for transfers between devices, body(): lax.all_to_all(jnp.stack([real_part, imag_part], axis=1), 'tm', split_axi...  25.8 us
    ppermute x6, waiting for transfers between devices, with_halo(): lax.ppermute(head, axis, [((i + 1) % count, i) for i in range(ends)])  23.4 us
    all_to_all x1, blocking collectives, body(): return lax.all_to_all(values, 'tm', split_axis=0, concat_axis=2, tiled=True)  20.4 us
  transfers between devices with their start and end apart: 20, of which 20 were waited for; matrix products, arithmetic and copies ran while one was open for 1% of the time, Pallas kernels for 0%

commit v1 on v0

--- a/solution.py
+++ b/solution.py
@@ -132,8 +132,16 @@
     phases = phase_table(slot_freqs, all_times)
     real_part = jnp.einsum("sn,nzxy->szxy", jnp.cos(phases), series, precision=highest)
     imag_part = -jnp.einsum("sn,nzxy->szxy", jnp.sin(phases), series, precision=highest)
-    spectrum = lax.all_to_all(
-        jnp.stack([real_part, imag_part], axis=1), "tm", split_axis=0, concat_axis=3, tiled=True
+    spectrum = jnp.concatenate(
+        lax.all_to_all(
+            jnp.stack(
+                jnp.split(jnp.stack([real_part, imag_part], axis=1), lax.axis_size("tm"), axis=0)
+            ),
+            "tm",
+            0,
+            0,
+        ),
+        axis=3,
     )
     solved = solve_together(spectrum, absorption, own_freqs, own_counts, longest)
     gathered = lax.all_to_all(solved, "tm", split_axis=3, concat_axis=0, tiled=True)

time: 343 us -> 351 us (1.023)
  other arithmetic: 32 us -> 42.2 us
    unnamed x0 -> x15, other arithmetic: none -> 9.66 us
where the time goes in v1:
time: 351 us; the launch traced here: 350 us
  waiting for transfers between devices  153 us (44%)
  starting transfers between devices  89.2 us (25%)
  blocking collectives  47.4 us (14%)
  other arithmetic  42.2 us (12%)
  local copies, waits for them, and re-layouts  10 us (3%)
  loops' own time  5.21 us (1%)
    all_to_all x6, starting transfers between devices, copy_for_each(): return lax.all_to_all(copies, axis, split_axis=0, concat_axis=0, tiled=True)  46.4 us
    all_to_all x6, waiting for transfers between devices, copy_for_each(): return lax.all_to_all(copies, axis, split_axis=0, concat_axis=0, tiled=True)  38.6 us
    ppermute x6, waiting for transfers between devices, with_halo(): lax.ppermute(tail, axis, [(i, (i + 1) % count) for i in range(ends)])  37.3 us
    all_to_all x1, waiting for transfers between devices, body(): lax.all_to_all(solved, 'tm', split_axis=3, concat_axis=0, tiled=True)  28 us
    all_to_all x1, blocking collectives, body(): lax.all_to_all(scaled, 'tm', split_axis=2, concat_axis=0, tiled=True)  27 us
    all_to_all x1, waiting for transfers between devices, body(): lax.all_to_all(jnp.stack(jnp.split(jnp.stack([real_part, imag_part], axis...  25.8 us
    ppermute x6, waiting for transfers between devices, with_halo(): lax.ppermute(head, axis, [((i + 1) % count, i) for i in range(ends)])  23.4 us
    all_to_all x1, blocking collectives, body(): return lax.all_to_all(values, 'tm', split_axis=0, concat_axis=2, tiled=True)  20.4 us
  transfers between devices with their start and end apart: 20, of which 20 were waited for; matrix products, arithmetic and copies ran while one was open for 1% of the time, Pallas kernels for 0%

profile of v1, /device:TPU:1, one launch (start us, length us, event | category | flops | bytes accessed | tf_op | source)
XLA Modules:
  0.0 350.2 jit_solution(7412452106764786136)
XLA Ops:
  1.5 27.0 %all_to_all.71 = f32[4,2,128,128]{3,0,1,2:T(4,128)S(1)} all-to-all(f32[4,2,128,128]{3,0,1,2:T(4,128)S(1)} %copy.54), channel_id=1, replica_groups=mesh['tm'=16,'space'=16] {'tm'}, dimensions={2} | all-to-all | bytes 1048576 | tf_op jit(solution)/shard_map/all_to_all | solution.py:131
  40.4 3.7 %all-to-all-start.2 = ((f32[16,4,2,2,8,128]{5,1,4,3,2,0:T(4,128)}), f32[16,4,2,2,8,128]{5,1,4,3,2,0:T(4,128)S(1)}, u32[]{:S(2)}, u32[]{:S(2)}) async-start(f32[16,4,2,2,8,128]{5,1,4,3,2,0:T(4,128)} %fusion.38), calls=%async_computation.2 | async-start | bytes 2097152 | tf_op jit(solution)/shard_map/all_to_all | solution.py:136
  45.6 25.8 %all-to-all-done.2 = f32[16,4,2,2,8,128]{5,1,4,3,2,0:T(4,128)S(1)} async-done(((f32[16,4,2,2,8,128]{5,1,4,3,2,0:T(4,128)}), f32[16,4,2,2,8,128]{5,1,4,3,2,0:T(4,128)S(1)}, u32[]{:S(2)}, u32[]{:S(2)}) %all-to-all-start.2) | async-done | bytes 1048608 | tf_op jit(solution)/shard_map/all_to_all | solution.py:136
  73.3 204.2 %while.20 = (s32[]{:T(128)}, f32[4,2,128,128]{3,2,1,0:T(8,128)}, f32[4,2,128,128]{3,2,1,0:T(8,128)}, f32[4,2,128,128]{3,2,1,0:T(8,128)S(1)}, f32[4,2,128,128]{3,...) while((s32[]{:T(128)}, f32[4,2,128,128]{3,2,1,0:T(8,128)}, ...), condition=%wide.region_6.7_spmd.clone.clone, body=%wide.region_1.6_spmd.clone.clone.sunk | while | flops 9175258 | bytes 25447364 | solution.py:108
  74.4 3.1 collective-permute-start
  77.5 1.3 collective-permute-start.1
  78.9 9.4 %collective-permute-done = f32[4,2,1,128,128]{4,3,2,0,1:T(8,128)S(1)} collective-permute-done((f32[4,2,1,128,128]{4,3,2,0,1:T(8,128)S(1)}, f32[4,2,1,128,128]{4,3,2,0,1:T(8,128)S(1)}, u32[]{:S(2)}, u32[]{:S(2)}) %collective-permute-start) | collective-permute-done | bytes 524320 | tf_op jit(solution)/shard_map/while/body/ppermute | solution.py:22
  88.4 4.1 %collective-permute-done.1 = f32[4,2,1,128,128]{4,3,2,0,1:T(8,128)S(1)} collective-permute-done((f32[4,2,1,128,128]{4,3,2,0,1:T(8,128)S(1)}, f32[4,2,1,128,128]{4,3,2,0,1:T(8,128)S(1)}, u32[]{:S(2)}, u32[]{:S(2)}) %collective-permute-start.1) | collective-permute-done | bytes 524320 | tf_op jit(solution)/shard_map/while/body/ppermute | solution.py:24
  94.5 8.3 %all-to-all-start = ((f32[16,1,12]{2,1,0:T(1,128)}), f32[16,1,12]{2,1,0:T(1,128)S(1)}, u32[]{:S(2)}, u32[]{:S(2)}) async-start(f32[16,1,12]{2,1,0:T(1,128)} %broadcast_in_dim.42), calls=%async_computation | async-start | bytes 16384 | tf_op jit(solution)/shard_map/while/body/all_to_all | solution.py:33
  102.8 6.4 %all-to-all-done = f32[16,1,12]{2,1,0:T(1,128)S(1)} async-done(((f32[16,1,12]{2,1,0:T(1,128)}), f32[16,1,12]{2,1,0:T(1,128)S(1)}, u32[]{:S(2)}, u32[]{:S(2)}) %all-to-all-start) | async-done | bytes 800 | tf_op jit(solution)/shard_map/while/body/all_to_all | solution.py:33
  109.3 2.8 add_subtract_fusion.2
  113.2 2.1 collective-permute-start
  115.3 1.3 collective-permute-start.1
  116.7 8.1 %collective-permute-done = f32[4,2,1,128,128]{4,3,2,0,1:T(8,128)S(1)} collective-permute-done((f32[4,2,1,128,128]{4,3,2,0,1:T(8,128)S(1)}, f32[4,2,1,128,128]{4,3,2,0,1:T(8,128)S(1)}, u32[]{:S(2)}, u32[]{:S(2)}) %collective-permute-start) | collective-permute-done | bytes 524320 | tf_op jit(solution)/shard_map/while/body/ppermute | solution.py:22
  124.8 3.9 %collective-permute-done.1 = f32[4,2,1,128,128]{4,3,2,0,1:T(8,128)S(1)} collective-permute-done((f32[4,2,1,128,128]{4,3,2,0,1:T(8,128)S(1)}, f32[4,2,1,128,128]{4,3,2,0,1:T(8,128)S(1)}, u32[]{:S(2)}, u32[]{:S(2)}) %collective-permute-start.1) | collective-permute-done | bytes 524320 | tf_op jit(solution)/shard_map/while/body/ppermute | solution.py:24
  130.7 7.8 %all-to-all-start = ((f32[16,1,12]{2,1,0:T(1,128)}), f32[16,1,12]{2,1,0:T(1,128)S(1)}, u32[]{:S(2)}, u32[]{:S(2)}) async-start(f32[16,1,12]{2,1,0:T(1,128)} %broadcast_in_dim.42), calls=%async_computation | async-start | bytes 16384 | tf_op jit(solution)/shard_map/while/body/all_to_all | solution.py:33
  138.5 6.4 %all-to-all-done = f32[16,1,12]{2,1,0:T(1,128)S(1)} async-done(((f32[16,1,12]{2,1,0:T(1,128)}), f32[16,1,12]{2,1,0:T(1,128)S(1)}, u32[]{:S(2)}, u32[]{:S(2)}) %all-to-all-start) | async-done | bytes 800 | tf_op jit(solution)/shard_map/while/body/all_to_all | solution.py:33
  145.0 2.8 add_subtract_fusion.2
  148.9 2.1 collective-permute-start
  151.0 1.3 collective-permute-start.1
  152.4 5.7 %collective-permute-done = f32[4,2,1,128,128]{4,3,2,0,1:T(8,128)S(1)} collective-permute-done((f32[4,2,1,128,128]{4,3,2,0,1:T(8,128)S(1)}, f32[4,2,1,128,128]{4,3,2,0,1:T(8,128)S(1)}, u32[]{:S(2)}, u32[]{:S(2)}) %collective-permute-start) | collective-permute-done | bytes 524320 | tf_op jit(solution)/shard_map/while/body/ppermute | solution.py:22
  158.1 3.9 %collective-permute-done.1 = f32[4,2,1,128,128]{4,3,2,0,1:T(8,128)S(1)} collective-permute-done((f32[4,2,1,128,128]{4,3,2,0,1:T(8,128)S(1)}, f32[4,2,1,128,128]{4,3,2,0,1:T(8,128)S(1)}, u32[]{:S(2)}, u32[]{:S(2)}) %collective-permute-start.1) | collective-permute-done | bytes 524320 | tf_op jit(solution)/shard_map/while/body/ppermute | solution.py:24
  164.0 7.8 %all-to-all-start = ((f32[16,1,12]{2,1,0:T(1,128)}), f32[16,1,12]{2,1,0:T(1,128)S(1)}, u32[]{:S(2)}, u32[]{:S(2)}) async-start(f32[16,1,12]{2,1,0:T(1,128)} %broadcast_in_dim.42), calls=%async_computation | async-start | bytes 16384 | tf_op jit(solution)/shard_map/while/body/all_to_all | solution.py:33
  171.8 6.4 %all-to-all-done = f32[16,1,12]{2,1,0:T(1,128)S(1)} async-done(((f32[16,1,12]{2,1,0:T(1,128)}), f32[16,1,12]{2,1,0:T(1,128)S(1)}, u32[]{:S(2)}, u32[]{:S(2)}) %all-to-all-start) | async-done | bytes 800 | tf_op jit(solution)/shard_map/while/body/all_to_all | solution.py:33
  178.3 2.8 add_subtract_fusion.2
  182.2 2.1 collective-permute-start
  185.7 4.7 %collective-permute-done = f32[4,2,1,128,128]{4,3,2,0,1:T(8,128)S(1)} collective-permute-done((f32[4,2,1,128,128]{4,3,2,0,1:T(8,128)S(1)}, f32[4,2,1,128,128]{4,3,2,0,1:T(8,128)S(1)}, u32[]{:S(2)}, u32[]{:S(2)}) %collective-permute-start) | collective-permute-done | bytes 524320 | tf_op jit(solution)/shard_map/while/body/ppermute | solution.py:22
  190.3 3.8 %collective-permute-done.1 = f32[4,2,1,128,128]{4,3,2,0,1:T(8,128)S(1)} collective-permute-done((f32[4,2,1,128,128]{4,3,2,0,1:T(8,128)S(1)}, f32[4,2,1,128,128]{4,3,2,0,1:T(8,128)S(1)}, u32[]{:S(2)}, u32[]{:S(2)}) %collective-permute-start.1) | collective-permute-done | bytes 524320 | tf_op jit(solution)/shard_map/while/body/ppermute | solution.py:24
  196.2 7.5 %all-to-all-start = ((f32[16,1,12]{2,1,0:T(1,128)}), f32[16,1,12]{2,1,0:T(1,128)S(1)}, u32[]{:S(2)}, u32[]{:S(2)}) async-start(f32[16,1,12]{2,1,0:T(1,128)} %broadcast_in_dim.42), calls=%async_computation | async-start | bytes 16384 | tf_op jit(solution)/shard_map/while/body/all_to_all | solution.py:33
  203.7 6.4 %all-to-all-done = f32[16,1,12]{2,1,0:T(1,128)S(1)} async-done(((f32[16,1,12]{2,1,0:T(1,128)}), f32[16,1,12]{2,1,0:T(1,128)S(1)}, u32[]{:S(2)}, u32[]{:S(2)}) %all-to-all-start) | async-done | bytes 800 | tf_op jit(solution)/shard_map/while/body/all_to_all | solution.py:33
  210.2 2.8 add_subtract_fusion.2
  214.1 2.1 collective-permute-start
  217.6 4.7 %collective-permute-done = f32[4,2,1,128,128]{4,3,2,0,1:T(8,128)S(1)} collective-permute-done((f32[4,2,1,128,128]{4,3,2,0,1:T(8,128)S(1)}, f32[4,2,1,128,128]{4,3,2,0,1:T(8,128)S(1)}, u32[]{:S(2)}, u32[]{:S(2)}) %collective-permute-start) | collective-permute-done | bytes 524320 | tf_op jit(solution)/shard_map/while/body/ppermute | solution.py:22
  222.3 3.8 %collective-permute-done.1 = f32[4,2,1,128,128]{4,3,2,0,1:T(8,128)S(1)} collective-permute-done((f32[4,2,1,128,128]{4,3,2,0,1:T(8,128)S(1)}, f32[4,2,1,128,128]{4,3,2,0,1:T(8,128)S(1)}, u32[]{:S(2)}, u32[]{:S(2)}) %collective-permute-start.1) | collective-permute-done | bytes 524320 | tf_op jit(solution)/shard_map/while/body/ppermute | solution.py:24
  228.1 7.5 %all-to-all-start = ((f32[16,1,12]{2,1,0:T(1,128)}), f32[16,1,12]{2,1,0:T(1,128)S(1)}, u32[]{:S(2)}, u32[]{:S(2)}) async-start(f32[16,1,12]{2,1,0:T(1,128)} %broadcast_in_dim.42), calls=%async_computation | async-start | bytes 16384 | tf_op jit(solution)/shard_map/while/body/all_to_all | solution.py:33
  235.6 6.4 %all-to-all-done = f32[16,1,12]{2,1,0:T(1,128)S(1)} async-done(((f32[16,1,12]{2,1,0:T(1,128)}), f32[16,1,12]{2,1,0:T(1,128)S(1)}, u32[]{:S(2)}, u32[]{:S(2)}) %all-to-all-start) | async-done | bytes 800 | tf_op jit(solution)/shard_map/while/body/all_to_all | solution.py:33
  242.2 2.8 add_subtract_fusion.2
  246.0 2.1 collective-permute-start
  249.5 4.7 %collective-permute-done = f32[4,2,1,128,128]{4,3,2,0,1:T(8,128)S(1)} collective-permute-done((f32[4,2,1,128,128]{4,3,2,0,1:T(8,128)S(1)}, f32[4,2,1,128,128]{4,3,2,0,1:T(8,128)S(1)}, u32[]{:S(2)}, u32[]{:S(2)}) %collective-permute-start) | collective-permute-done | bytes 524320 | tf_op jit(solution)/shard_map/while/body/ppermute | solution.py:22
  254.2 3.8 %collective-permute-done.1 = f32[4,2,1,128,128]{4,3,2,0,1:T(8,128)S(1)} collective-permute-done((f32[4,2,1,128,128]{4,3,2,0,1:T(8,128)S(1)}, f32[4,2,1,128,128]{4,3,2,0,1:T(8,128)S(1)}, u32[]{:S(2)}, u32[]{:S(2)}) %collective-permute-start.1) | collective-permute-done | bytes 524320 | tf_op jit(solution)/shard_map/while/body/ppermute | solution.py:24
  260.0 7.5 %all-to-all-start = ((f32[16,1,12]{2,1,0:T(1,128)}), f32[16,1,12]{2,1,0:T(1,128)S(1)}, u32[]{:S(2)}, u32[]{:S(2)}) async-start(f32[16,1,12]{2,1,0:T(1,128)} %broadcast_in_dim.42), calls=%async_computation | async-start | bytes 16384 | tf_op jit(solution)/shard_map/while/body/all_to_all | solution.py:33
  267.5 6.4 %all-to-all-done = f32[16,1,12]{2,1,0:T(1,128)S(1)} async-done(((f32[16,1,12]{2,1,0:T(1,128)}), f32[16,1,12]{2,1,0:T(1,128)S(1)}, u32[]{:S(2)}, u32[]{:S(2)}) %all-to-all-start) | async-done | bytes 800 | tf_op jit(solution)/shard_map/while/body/all_to_all | solution.py:33
  274.1 2.8 add_subtract_fusion.2
  277.5 2.0 copy_bitcast_fusion.2
  279.6 1.5 pad_maximum_fusion.6
  281.0 17.8 %all-to-all-start.3 = ((f32[4,2,2,128,128]{4,2,0,1,3:T(2,128)}), f32[4,2,2,128,128]{4,2,0,1,3:T(2,128)S(1)}, u32[]{:S(2)}, u32[]{:S(2)}) async-start(f32[4,2,2,128,128]{4,2,0,1,3:T(2,128)} %pad_maximum_fusion.6), calls=%async_computation.3 | async-start | bytes 2097152 | tf_op jit(solution)/shard_map/all_to_all | solution.py:147
  298.9 28.0 %all-to-all-done.3 = f32[4,2,2,128,128]{4,2,0,1,3:T(2,128)S(1)} async-done(((f32[4,2,2,128,128]{4,2,0,1,3:T(2,128)}), f32[4,2,2,128,128]{4,2,0,1,3:T(2,128)S(1)}, u32[]{:S(2)}, u32[]{:S(2)}) %all-to-all-start.3) | async-done | bytes 1048608 | tf_op jit(solution)/shard_map/all_to_all | solution.py:147
  328.9 20.4 %all_to_all.72 = f32[64,2,8,128]{3,2,1,0:T(8,128)S(1)} all-to-all(f32[64,2,8,128]{3,2,1,0:T(8,128)S(1)} %copy.60), channel_id=1, replica_groups=mesh['tm'=16,'space'=16] {'tm'}, dimensions={0} | all-to-all | bytes 1048576 | tf_op jit(solution)/shard_map/all_to_all | solution.py:155
  (100 shorter events, 38.9 us)
Async XLA Ops:
  40.4 3.9 %copy-start = (s32[64]{0:T(128)S(1)}, s32[64]{0:T(128)}, u32[]{:S(2)}) copy-start(s32[64]{0:T(128)} %param.7) | copy-start | bytes 772
  40.4 31.1 %all-to-all-start.2 = ((f32[16,4,2,2,8,128]{5,1,4,3,2,0:T(4,128)}), f32[16,4,2,2,8,128]{5,1,4,3,2,0:T(4,128)S(1)}, u32[]{:S(2)}, u32[]{:S(2)}) async-start(f32[16,4,2,2,8,128]{5,1,4,3,2,0:T(4,128)} %fusion.38), calls=%async_computation.2 | async-start | bytes 2097152 | tf_op jit(solution)/shard_map/all_to_all | solution.py:136
  71.6 1.7 copy-start.1
  74.4 14.0 %collective-permute-start = (f32[4,2,1,128,128]{4,3,2,0,1:T(8,128)S(1)}, f32[4,2,1,128,128]{4,3,2,0,1:T(8,128)S(1)}, u32[]{:S(2)}, u32[]{:S(2)}) collective-permute-start(f32[4,2,1,128,128]{4,3,2,0,1:T(8,128)S(1)} %get-tuple-element.368), channel_id=1, source_target_pairs={{0,1},{1,2},{2,3},{3,4},{4,5},{5,6},{6,7},{7,8},{8,9},{9,10},{10,1... | collective-permute-start | bytes 1572872 | tf_op jit(solution)/shard_map/while/body/ppermute | solution.py:22
  77.5 15.0 %collective-permute-start.1 = (f32[4,2,1,128,128]{4,3,2,0,1:T(8,128)S(1)}, f32[4,2,1,128,128]{4,3,2,0,1:T(8,128)S(1)}, u32[]{:S(2)}, u32[]{:S(2)}) collective-permute-start(f32[4,2,1,128,128]{4,3,2,0,1:T(8,128)S(1)} %get-tuple-element.369), channel_id=1, source_target_pairs={{1,0},{2,1},{3,2},{4,3},{5,4},{6,5},{7,6},{8,7},{9,8},{10,9},{11,1... | collective-permute-start | bytes 1572872 | tf_op jit(solution)/shard_map/while/body/ppermute | solution.py:24
  94.5 14.7 %all-to-all-start = ((f32[16,1,12]{2,1,0:T(1,128)}), f32[16,1,12]{2,1,0:T(1,128)S(1)}, u32[]{:S(2)}, u32[]{:S(2)}) async-start(f32[16,1,12]{2,1,0:T(1,128)} %broadcast_in_dim.42), calls=%async_computation | async-start | bytes 16384 | tf_op jit(solution)/shard_map/while/body/all_to_all | solution.py:33
  113.2 11.6 %collective-permute-start = (f32[4,2,1,128,128]{4,3,2,0,1:T(8,128)S(1)}, f32[4,2,1,128,128]{4,3,2,0,1:T(8,128)S(1)}, u32[]{:S(2)}, u32[]{:S(2)}) collective-permute-start(f32[4,2,1,128,128]{4,3,2,0,1:T(8,128)S(1)} %get-tuple-element.368), channel_id=1, source_target_pairs={{0,1},{1,2},{2,3},{3,4},{4,5},{5,6},{6,7},{7,8},{8,9},{9,10},{10,1... | collective-permute-start | bytes 1572872 | tf_op jit(solution)/shard_map/while/body/ppermute | solution.py:22
  115.3 13.4 %collective-permute-start.1 = (f32[4,2,1,128,128]{4,3,2,0,1:T(8,128)S(1)}, f32[4,2,1,128,128]{4,3,2,0,1:T(8,128)S(1)}, u32[]{:S(2)}, u32[]{:S(2)}) collective-permute-start(f32[4,2,1,128,128]{4,3,2,0,1:T(8,128)S(1)} %get-tuple-element.369), channel_id=1, source_target_pairs={{1,0},{2,1},{3,2},{4,3},{5,4},{6,5},{7,6},{8,7},{9,8},{10,9},{11,1... | collective-permute-start | bytes 1572872 | tf_op jit(solution)/shard_map/while/body/ppermute | solution.py:24
  130.7 14.3 %all-to-all-start = ((f32[16,1,12]{2,1,0:T(1,128)}), f32[16,1,12]{2,1,0:T(1,128)S(1)}, u32[]{:S(2)}, u32[]{:S(2)}) async-start(f32[16,1,12]{2,1,0:T(1,128)} %broadcast_in_dim.42), calls=%async_computation | async-start | bytes 16384 | tf_op jit(solution)/shard_map/while/body/all_to_all | solution.py:33
  148.9 9.2 %collective-permute-start = (f32[4,2,1,128,128]{4,3,2,0,1:T(8,128)S(1)}, f32[4,2,1,128,128]{4,3,2,0,1:T(8,128)S(1)}, u32[]{:S(2)}, u32[]{:S(2)}) collective-permute-start(f32[4,2,1,128,128]{4,3,2,0,1:T(8,128)S(1)} %get-tuple-element.368), channel_id=1, source_target_pairs={{0,1},{1,2},{2,3},{3,4},{4,5},{5,6},{6,7},{7,8},{8,9},{9,10},{10,1... | collective-permute-start | bytes 1572872 | tf_op jit(solution)/shard_map/while/body/ppermute | solution.py:22
  151.0 11.0 %collective-permute-start.1 = (f32[4,2,1,128,128]{4,3,2,0,1:T(8,128)S(1)}, f32[4,2,1,128,128]{4,3,2,0,1:T(8,128)S(1)}, u32[]{:S(2)}, u32[]{:S(2)}) collective-permute-start(f32[4,2,1,128,128]{4,3,2,0,1:T(8,128)S(1)} %get-tuple-element.369), channel_id=1, source_target_pairs={{1,0},{2,1},{3,2},{4,3},{5,4},{6,5},{7,6},{8,7},{9,8},{10,9},{11,1... | collective-permute-start | bytes 1572872 | tf_op jit(solution)/shard_map/while/body/ppermute | solution.py:24
  164.0 14.3 %all-to-all-start = ((f32[16,1,12]{2,1,0:T(1,128)}), f32[16,1,12]{2,1,0:T(1,128)S(1)}, u32[]{:S(2)}, u32[]{:S(2)}) async-start(f32[16,1,12]{2,1,0:T(1,128)} %broadcast_in_dim.42), calls=%async_computation | async-start | bytes 16384 | tf_op jit(solution)/shard_map/while/body/all_to_all | solution.py:33
  182.2 8.2 %collective-permute-start = (f32[4,2,1,128,128]{4,3,2,0,1:T(8,128)S(1)}, f32[4,2,1,128,128]{4,3,2,0,1:T(8,128)S(1)}, u32[]{:S(2)}, u32[]{:S(2)}) collective-permute-start(f32[4,2,1,128,128]{4,3,2,0,1:T(8,128)S(1)} %get-tuple-element.368), channel_id=1, source_target_pairs={{0,1},{1,2},{2,3},{3,4},{4,5},{5,6},{6,7},{7,8},{8,9},{9,10},{10,1... | collective-permute-start | bytes 1572872 | tf_op jit(solution)/shard_map/while/body/ppermute | solution.py:22
  184.3 9.9 %collective-permute-start.1 = (f32[4,2,1,128,128]{4,3,2,0,1:T(8,128)S(1)}, f32[4,2,1,128,128]{4,3,2,0,1:T(8,128)S(1)}, u32[]{:S(2)}, u32[]{:S(2)}) collective-permute-start(f32[4,2,1,128,128]{4,3,2,0,1:T(8,128)S(1)} %get-tuple-element.369), channel_id=1, source_target_pairs={{1,0},{2,1},{3,2},{4,3},{5,4},{6,5},{7,6},{8,7},{9,8},{10,9},{11,1... | collective-permute-start | bytes 1572872 | tf_op jit(solution)/shard_map/while/body/ppermute | solution.py:24
  196.2 14.0 %all-to-all-start = ((f32[16,1,12]{2,1,0:T(1,128)}), f32[16,1,12]{2,1,0:T(1,128)S(1)}, u32[]{:S(2)}, u32[]{:S(2)}) async-start(f32[16,1,12]{2,1,0:T(1,128)} %broadcast_in_dim.42), calls=%async_computation | async-start | bytes 16384 | tf_op jit(solution)/shard_map/while/body/all_to_all | solution.py:33
  214.1 8.2 %collective-permute-start = (f32[4,2,1,128,128]{4,3,2,0,1:T(8,128)S(1)}, f32[4,2,1,128,128]{4,3,2,0,1:T(8,128)S(1)}, u32[]{:S(2)}, u32[]{:S(2)}) collective-permute-start(f32[4,2,1,128,128]{4,3,2,0,1:T(8,128)S(1)} %get-tuple-element.368), channel_id=1, source_target_pairs={{0,1},{1,2},{2,3},{3,4},{4,5},{5,6},{6,7},{7,8},{8,9},{9,10},{10,1... | collective-permute-start | bytes 1572872 | tf_op jit(solution)/shard_map/while/body/ppermute | solution.py:22
  216.2 9.9 %collective-permute-start.1 = (f32[4,2,1,128,128]{4,3,2,0,1:T(8,128)S(1)}, f32[4,2,1,128,128]{4,3,2,0,1:T(8,128)S(1)}, u32[]{:S(2)}, u32[]{:S(2)}) collective-permute-start(f32[4,2,1,128,128]{4,3,2,0,1:T(8,128)S(1)} %get-tuple-element.369), channel_id=1, source_target_pairs={{1,0},{2,1},{3,2},{4,3},{5,4},{6,5},{7,6},{8,7},{9,8},{10,9},{11,1... | collective-permute-start | bytes 1572872 | tf_op jit(solution)/shard_map/while/body/ppermute | solution.py:24
  228.1 14.0 %all-to-all-start = ((f32[16,1,12]{2,1,0:T(1,128)}), f32[16,1,12]{2,1,0:T(1,128)S(1)}, u32[]{:S(2)}, u32[]{:S(2)}) async-start(f32[16,1,12]{2,1,0:T(1,128)} %broadcast_in_dim.42), calls=%async_computation | async-start | bytes 16384 | tf_op jit(solution)/shard_map/while/body/all_to_all | solution.py:33
  246.0 8.2 %collective-permute-start = (f32[4,2,1,128,128]{4,3,2,0,1:T(8,128)S(1)}, f32[4,2,1,128,128]{4,3,2,0,1:T(8,128)S(1)}, u32[]{:S(2)}, u32[]{:S(2)}) collective-permute-start(f32[4,2,1,128,128]{4,3,2,0,1:T(8,128)S(1)} %get-tuple-element.368), channel_id=1, source_target_pairs={{0,1},{1,2},{2,3},{3,4},{4,5},{5,6},{6,7},{7,8},{8,9},{9,10},{10,1... | collective-permute-start | bytes 1572872 | tf_op jit(solution)/shard_map/while/body/ppermute | solution.py:22
  248.1 9.9 %collective-permute-start.1 = (f32[4,2,1,128,128]{4,3,2,0,1:T(8,128)S(1)}, f32[4,2,1,128,128]{4,3,2,0,1:T(8,128)S(1)}, u32[]{:S(2)}, u32[]{:S(2)}) collective-permute-start(f32[4,2,1,128,128]{4,3,2,0,1:T(8,128)S(1)} %get-tuple-element.369), channel_id=1, source_target_pairs={{1,0},{2,1},{3,2},{4,3},{5,4},{6,5},{7,6},{8,7},{9,8},{10,9},{11,1... | collective-permute-start | bytes 1572872 | tf_op jit(solution)/shard_map/while/body/ppermute | solution.py:24
  260.0 14.0 %all-to-all-start = ((f32[16,1,12]{2,1,0:T(1,128)}), f32[16,1,12]{2,1,0:T(1,128)S(1)}, u32[]{:S(2)}, u32[]{:S(2)}) async-start(f32[16,1,12]{2,1,0:T(1,128)} %broadcast_in_dim.42), calls=%async_computation | async-start | bytes 16384 | tf_op jit(solution)/shard_map/while/body/all_to_all | solution.py:33
  281.0 45.9 %all-to-all-start.3 = ((f32[4,2,2,128,128]{4,2,0,1,3:T(2,128)}), f32[4,2,2,128,128]{4,2,0,1,3:T(2,128)S(1)}, u32[]{:S(2)}, u32[]{:S(2)}) async-start(f32[4,2,2,128,128]{4,2,0,1,3:T(2,128)} %pad_maximum_fusion.6), calls=%async_computation.3 | async-start | bytes 2097152 | tf_op jit(solution)/shard_map/all_to_all | solution.py:147
